TPU v7x, 32 devices: a whole 2x2x4 slice. The times are simulated.
32 devices in a mesh: dp: 4 (over z), ctx: 4 (over y, core), tp: 2 (over x).
Axes of the slice: x: 2, y: 2, z: 4, core: 2. Of those that a mesh axis runs over, the one named last changes fastest.
Arguments:
- queries: bfloat16 [4, 512, 4096], P('dp', 'ctx', 'tp'), may hold values from -8 to 8
- keys_text: bfloat16 [4, 512, 512], P('dp', 'ctx', 'tp'), may hold values from -8 to 8
- values_text: bfloat16 [4, 512, 512], P('dp', 'ctx', 'tp'), may hold values from -6 to 6
- patch_rows: bfloat16 [4, 4, 8, 2, 512], P('dp', 'ctx', None, None, 'tp'), may hold values from -6 to 6
- patch_owner: int32 [4, 4, 8, 1], P('dp', 'ctx'), may hold values from 0 to 3; in each aligned block of 8 rows (0 to 7, 8 to 15, ..., all dimensions but the last counted through in order) at most 4 rows name the same one
- patch_place: int32 [4, 4, 8], P('dp', 'ctx'), may hold values from 0 to 127
- value_head: bfloat16 [4096], P('tp'), may hold values from -0.75 to 0.75
Outputs:
- attention: bfloat16 [4, 512, 4096], P('dp', 'ctx', 'tp')
- value_out: float32 [4, 512], P('dp', 'ctx')
Inputs may be any that keep to these rules, and one draw needn't show every extreme that they name: `patch_owner`: among the rows of one vision shard at most 4 name the same sequence, and exactly 4 do in some shards. `patch_place`: rows that share an owner, a ctx index and a position are all added there.
All inputs are finite; a program needn't handle non-finite values.
Results may differ from a plain program's by a relative error of at most 0.0079.
Values may be sent and summed in bfloat16 or wider, within the bound.
A program may use at most 64 MiB of HBM per device.

v0:
```python
import jax
import jax.numpy as jnp
from jax import lax
from jax.sharding import PartitionSpec as P

HD = 128
CAP = 4


def attend_block(
    carried, query_split, query_place, block_keys, block_values, key_place, score_scale
):
    running_max, denominator, numerator = carried
    scores = (
        jnp.einsum("tgrd,sgd->tgrs", query_split, block_keys, preferred_element_type=jnp.float32)
        * score_scale
    )
    allowed = (key_place[None, :] <= query_place[:, None])[:, None, None, :]
    scores = jnp.where(allowed, scores, -1e30)
    new_max = jnp.maximum(running_max, jnp.max(scores, axis=-1))
    weights = jnp.where(allowed, jnp.exp(scores - new_max[..., None]), 0.0)
    shrink = jnp.exp(running_max - new_max)
    denominator = denominator * shrink + jnp.sum(weights, axis=-1)
    numerator = numerator * shrink[..., None] + jnp.einsum(
        "tgrs,sgd->tgrd",
        weights.astype(jnp.bfloat16),
        block_values,
        preferred_element_type=jnp.float32,
    )
    return (new_max, denominator, numerator)


def unchanged(carried):
    return carried


def body(queries, keys_text, values_text, patch_rows, patch_owner, patch_place, value_head):
    token_count = queries.shape[1]
    kv_width = keys_text.shape[2]
    groups = kv_width // HD
    head_count = queries.shape[2] // HD
    group_size = head_count // groups
    score_scale = HD ** (-0.5)
    dp_count = lax.axis_size("dp")
    slot_count = dp_count * CAP
    owner_seq = patch_owner[0, 0, :, 0]
    places = patch_place[0, 0]
    owner_hits = (owner_seq[:, None] == jnp.arange(dp_count, dtype=jnp.int32)[None, :]).astype(
        jnp.int32
    )
    before = jnp.cumsum(owner_hits, axis=0) - owner_hits
    slot_rank = jnp.sum(before * owner_hits, axis=1)
    target = owner_seq * CAP + slot_rank
    select = (jnp.arange(slot_count, dtype=jnp.int32)[:, None] == target[None, :]).astype(jnp.int32)
    row_data = patch_rows[0, 0].reshape(places.shape[0], 2 * kv_width)
    packed = jnp.dot(
        select.astype(jnp.bfloat16), row_data, preferred_element_type=jnp.float32
    ).astype(jnp.bfloat16)
    filled = jnp.sum(select, axis=1)
    slot_place = jnp.sum(select * places[None, :], axis=1) + (1 - filled) * token_count
    packed = packed.reshape(slot_count, 2, kv_width)
    arrived, arrived_place = (
        lax.all_to_all(packed, "dp", split_axis=0, concat_axis=0, tiled=True),
        lax.all_to_all(slot_place, "dp", split_axis=0, concat_axis=0, tiled=True),
    )
    landing = (jnp.arange(token_count, dtype=jnp.int32)[:, None] == arrived_place[None, :]).astype(
        jnp.bfloat16
    )
    arrivals = jnp.dot(
        landing, arrived.reshape(slot_count, 2 * kv_width), preferred_element_type=jnp.float32
    )
    merged_keys = (keys_text[0].astype(jnp.float32) + arrivals[:, :kv_width]).astype(jnp.bfloat16)
    merged_values = (values_text[0].astype(jnp.float32) + arrivals[:, kv_width:]).astype(
        jnp.bfloat16
    )
    query_split = queries[0].reshape(token_count, groups, group_size, HD)
    first_row = lax.axis_index("ctx") * token_count
    query_place = first_row + jnp.arange(token_count, dtype=jnp.int32)
    initial = (
        jnp.full((token_count, groups, group_size), -1e30, jnp.float32),
        jnp.zeros((token_count, groups, group_size), jnp.float32),
        jnp.zeros((token_count, groups, group_size, HD), jnp.float32),
    )
    carried = initial
    start_row = jnp.int32(0)
    piece_keys = lax.all_gather(merged_keys, "ctx", axis=0, tiled=True)
    piece_values = lax.all_gather(merged_values, "ctx", axis=0, tiled=True)
    piece_rows = piece_keys.shape[0]
    block_rows = min(512, piece_rows)
    for lower in range(0, piece_rows, block_rows):
        upper = min(lower + block_rows, piece_rows)
        block_keys = piece_keys[lower:upper].reshape(upper - lower, groups, HD)
        block_values = piece_values[lower:upper].reshape(upper - lower, groups, HD)
        key_place = start_row + lower + jnp.arange(upper - lower, dtype=jnp.int32)

        def update(state_in):
            return attend_block(
                state_in, query_split, query_place, block_keys, block_values, key_place, score_scale
            )

        carried = lax.cond(
            start_row + lower <= first_row + token_count - 1, update, unchanged, carried
        )
    running_max, denominator, numerator = carried
    attention = (
        (numerator / denominator[..., None])
        .reshape(token_count, head_count * HD)
        .astype(jnp.bfloat16)
    )
    partial_value = jnp.dot(attention, value_head, preferred_element_type=jnp.float32)
    value_out = lax.psum(partial_value, "tp")
    return (attention[None], value_out[None])


def solution(mesh):
    in_specs = (
        P("dp", "ctx", "tp"),
        P("dp", "ctx", "tp"),
        P("dp", "ctx", "tp"),
        P("dp", "ctx", None, None, "tp"),
        P("dp", "ctx", None, None),
        P("dp", "ctx", None),
        P("tp"),
    )
    out_specs = (P("dp", "ctx", "tp"), P("dp", "ctx"))
    return jax.shard_map(body, mesh=mesh, in_specs=in_specs, out_specs=out_specs, check_vma=False)
```

profile of v0, /device:TPU:0, one launch (start us, length us, event | category | flops | bytes accessed | tf_op | source)
XLA Modules:
  0.0 53.5 jit_solution(15466480431015100622)
XLA Ops:
  0.6 0.7 %fusion.25 = s32[8,4]{0,1:T(4,128)S(1)} fusion(s32[8]{0:T(128)} %bitcast.58), kind=kLoop, calls=%fused_computation.37 | loop fusion | flops 64 | bytes 160 | tf_op jit(solution)/shard_map/convert_element_type | solution.py:48
  1.3 0.2 reduce_window_sum.11
  1.5 0.7 %select_reduce_fusion.1 = s32[8]{0:T(128)S(1)} fusion(s32[8,4]{0,1:T(4,128)S(1)} %reduce_window_sum.11, s32[8]{0:T(128)} %bitcast.59), kind=kLoop, calls=%fused_computation.35 | loop fusion | flops 152 | bytes 192 | tf_op jit(solution)/shard_map/reduce_sum | solution.py:52
  2.2 0.7 %multiply_add_fusion.1 = s32[8]{0:T(128)S(1)} fusion(s32[8]{0:T(128)S(1)} %select_reduce_fusion.1, s32[1,1,8,1]{2,3,1,0:T(1,128)} %param.13), kind=kLoop, calls=%fused_computation.39 | loop fusion | flops 16 | bytes 96 | tf_op jit(solution)/shard_map/add | solution.py:53
  2.8 0.7 %convert_reduce_fusion = (s32[16]{0:T(128)S(1)}, s32[16]{0:T(128)S(1)}) fusion(s32[8]{0:T(128)S(1)} %multiply_add_fusion.1, s32[8]{0:T(128)} %bitcast.60), kind=kLoop, calls=%fused_computation.31 | loop fusion | flops 608 | bytes 192 | tf_op jit(solution)/shard_map/reduce_sum | solution.py:59
  3.6 0.7 %add.48 = s32[4,4,1]{1,0,2:T(4,128)} reshape(s32[16]{0:T(128)S(1)} %multiply_add_fusion) | data formatting | bytes 128 | tf_op jit(solution)/shard_map/add | solution.py:60
  4.2 6.3 %all-to-all-start = ((s32[4,4,1]{1,2,0:T(1,128)}), s32[4,4,1]{1,2,0:T(1,128)S(1)}, u32[]{:S(2)}, u32[]{:S(2)}) async-start(s32[4,4,1]{1,2,0:T(1,128)} %bitcast.7), calls=%async_computation | async-start | bytes 4096 | tf_op jit(solution)/shard_map/all_to_all | solution.py:64
  10.6 0.7 %copy.45 = bf16[1,8,2,256]{3,1,2,0:T(8,128)(2,1)S(1)} copy(bf16[1,8,2,256]{3,2,1,0:T(2,128)(2,1)} %bitcast.56) | data formatting | bytes 16384
  11.3 0.3 convolution_convert_fusion
  11.5 0.6 %reshape.108 = bf16[16,2,256]{2,1,0:T(2,128)(2,1)} reshape(bf16[16,512]{1,0:T(8,128)(2,1)S(1)} %convolution_convert_fusion) | data formatting | bytes 32768 | tf_op jit(solution)/shard_map/reshape | solution.py:61
  12.2 3.8 %all-to-all-done = s32[4,4,1]{1,2,0:T(1,128)S(1)} async-done(((s32[4,4,1]{1,2,0:T(1,128)}), s32[4,4,1]{1,2,0:T(1,128)S(1)}, u32[]{:S(2)}, u32[]{:S(2)}) %all-to-all-start) | async-done | bytes 96 | tf_op jit(solution)/shard_map/all_to_all | solution.py:64
  16.0 3.3 %all-to-all-start.1 = ((bf16[16,2,256]{2,1,0:T(2,128)(2,1)}), bf16[16,2,256]{2,1,0:T(2,128)(2,1)S(1)}, u32[]{:S(2)}, u32[]{:S(2)}) async-start(bf16[16,2,256]{2,1,0:T(2,128)(2,1)} %reshape.108), calls=%async_computation.1 | async-start | bytes 32768 | tf_op jit(solution)/shard_map/all_to_all | solution.py:63
  19.3 0.7 %reshape.114 = bf16[2048,1]{0,1:T(2,128)(2,1)S(1)} reshape(bf16[2048]{0:T(1024)(128)(2,1)} %param.15) | data formatting | bytes 8192 | tf_op args[6]
  20.0 0.6 %broadcast.91 = s32[]{:T(128)} broadcast(s32[]{:T(128)} %constant.11.clone.1), dimensions={} | broadcast | bytes 8 | tf_op jit(solution)/shard_map/all_to_all | solution.py:64
  20.6 0.7 %reduce.3 = s32[4,4]{1,0:T(4,128)S(1)} reduce(s32[4,4,1]{1,2,0:T(1,128)S(1)} %all-to-all-done, s32[]{:T(128)} %broadcast.91), dimensions={2}, to_apply=%all_to_all.7.reduce_sub_computation.3 | reduce | bytes 132 | tf_op jit(solution)/shard_map/all_to_all | solution.py:64
  21.3 0.1 eq.48
  21.4 3.5 %all-to-all-done.1 = bf16[16,2,256]{2,1,0:T(2,128)(2,1)S(1)} async-done(((bf16[16,2,256]{2,1,0:T(2,128)(2,1)}), bf16[16,2,256]{2,1,0:T(2,128)(2,1)S(1)}, u32[]{:S(2)}, u32[]{:S(2)}) %all-to-all-start.1) | async-done | bytes 16416 | tf_op jit(solution)/shard_map/all_to_all | solution.py:63
  24.9 0.2 fusion.22
  25.0 0.9 %fusion.20 = (bf16[128,256]{1,0:T(8,128)(2,1)S(1)}, bf16[128,256]{1,0:T(8,128)(2,1)S(1)}) fusion(f32[128,512]{1,0:T(8,128)S(1)} %fusion.22, bf16[1,128,256]{2,1,0:T(8,128)(2,1)} %param.11, bf16[1,128,256]{2,1,0:T(8,128)(2,1)} %param.10), kind=kLoop, calls=%fused_computation.24 | loop fusion | flops 196608 | bytes 524288 | tf_op jit(solution)/shard_map/convert_element_type | solution.py:73
  25.9 5.8 %all_gather.6 = bf16[512,256]{1,0:T(8,128)(2,1)S(1)} all-gather(bf16[128,256]{1,0:T(8,128)(2,1)S(1)} %get-tuple-element.45), channel_id=1, replica_groups=mesh['dp'=4,'ctx'=4,'tp'=2] {'ctx'}, dimensions={0}, use_global_device_ids=true | all-gather | bytes 327680 | tf_op jit(solution)/shard_map/all_gather | solution.py:86
  31.7 5.8 %all_gather.7 = bf16[512,256]{1,0:T(8,128)(2,1)S(1)} all-gather(bf16[128,256]{1,0:T(8,128)(2,1)S(1)} %get-tuple-element.44), channel_id=1, replica_groups=mesh['dp'=4,'ctx'=4,'tp'=2] {'ctx'}, dimensions={0}, use_global_device_ids=true | all-gather | bytes 327680 | tf_op jit(solution)/shard_map/all_gather | solution.py:87
  37.6 9.2 %conditional.1 = (f32[128,2,8]{0,2,1:T(8,128)S(1)}, f32[128,2,8,128]{0,3,2,1:T(8,128)S(1)}) conditional(s32[]{:T(128)} %convert_element_type.53, () %tuple.16, (s32[512]{0:T(512)S(1)}, s32[]{:T(128)}, s32[128]{0:T(128)S(1)}, bf16[512,256]{1,0:T(8,128)(2,1)S(1)}, bf16[1,128,2048]{2,1,0:T(8,128)(2,1)}, /*index=5*/bf16[512,256]{1,0:T(8,128)(2,1)S(1)}) %tuple.17), branch_computations={%region_4.5_spmd, %region_5.8_spmd} | conditional | flops 550836352 | bytes 36007472 | solution.py:101
  37.6 0.1 broadcast_compare_fusion
  37.7 1.1 %copy.44 = bf16[16,8,16,128]{3,2,1,0:T(8,128)(2,1)S(1)} copy(bf16[16,8,16,128]{3,1,2,0:T(8,128)(2,1)} %bitcast.52) | data formatting | bytes 1048576 | tf_op jit(solution)/shard_map/cond
  38.9 0.1 reshape.104
  38.9 0.8 %fusion = (f32[128,2,8]{0,2,1:T(8,128)S(1)}, f32[2,512,128,8]{2,1,3,0:T(8,128)S(1)}) fusion(pred[128,512]{0,1:T(8,128)(4,1)S(1)} %broadcast_compare_fusion, bf16[128,2,8,128]{3,2,1,0:T(8,128)(2,1)S(1)} %bitcast.50, bf16[512,2,128,1]{2,1,0,3:T(2,128)(2,1)S(1)} %bitcast.51), kind=kOutput, calls=%fused_computation.2 | convolution fusion | flops 271579136 | bytes 5054464 | tf_op jit(solution)/shard_map/cond/branch_1_fun/tgrd,sgd->tgrs/dot_general | solution.py:15
  39.7 0.0 copy-start
  39.7 1.9 %copy-done = f32[2,512,128,8]{2,1,3,0:T(8,128)} copy-done((f32[2,512,128,8]{2,1,3,0:T(8,128)}, f32[2,512,128,8]{2,1,3,0:T(8,128)S(1)}, u32[]{:S(2)}) %copy-start) | copy-done | bytes 4194328 | tf_op jit(solution)/shard_map/cond
  41.7 1.0 %fusion.2 = f32[128,2,8]{0,2,1:T(8,128)S(1)} fusion(f32[2,512,128,8]{2,1,3,0:T(8,128)S(1)} %get-tuple-element.43, f32[128,2,8]{0,2,1:T(8,128)S(1)} %broadcast_maximum_fusion, pred[128,512]{0,1:T(8,128)(4,1)S(1)} %broadcast_compare_fusion), kind=kLoop, calls=%fused_computation.4 | loop fusion | flops 5240832 | bytes 4276224 | tf_op jit(solution)/shard_map/cond/branch_1_fun/reduce_sum | solution.py:23
  42.7 0.1 reshape.105
  42.8 3.7 %fusion.9 = f32[128,2,8,128]{3,0,2,1:T(8,128)S(1)} fusion(f32[2,512,128,8]{2,1,3,0:T(8,128)} %copy-done, f32[128,2,8]{0,2,1:T(8,128)S(1)} %broadcast_maximum_fusion, pred[128,512]{0,1:T(8,128)(4,1)S(1)} %broadcast_compare_fusion, f32[128,2,8]{0,2,1:T(8,128)S(1)} %get-tuple-element.40, bf16[512,2,128,1]{2,1,0,3:T(2,128)(2,1)S(1)} %bitcast.53), kind=kOutput, calls=%fused_computation.8 | convolution fusion | flops 273940480 | bytes 5586944 | tf_op jit(solution)/shard_map/cond/branch_1_fun/tgrs,sgd->tgrd/dot_general | solution.py:24
  46.5 0.3 copy.43
  46.8 0.1 divide_convert_fusion
  46.9 1.0 %copy.34 = bf16[1,128,2048]{2,1,0:T(8,128)(2,1)} copy(bf16[1,128,2048]{1,2,0:T(8,128)(2,1)S(1)} %bitcast.48) | data formatting | bytes 1048576
  47.9 0.2 fusion.26
  48.1 5.4 %psum.7 = f32[1,128]{1,0:T(1,128)} all-reduce(f32[1,128]{1,0:T(1,128)S(1)} %fusion.26), channel_id=1, replica_groups=mesh['dp'=4,'ctx'=4,'tp'=2] {'tp'}, use_global_device_ids=true, to_apply=%region_8.9 | all-reduce | flops 128 | bytes 1024 | tf_op jit(solution)/shard_map/psum | solution.py:111
  (7 shorter events, 0.0 us)
Async XLA Ops:
  4.2 11.8 %all-to-all-start = ((s32[4,4,1]{1,2,0:T(1,128)}), s32[4,4,1]{1,2,0:T(1,128)S(1)}, u32[]{:S(2)}, u32[]{:S(2)}) async-start(s32[4,4,1]{1,2,0:T(1,128)} %bitcast.7), calls=%async_computation | async-start | bytes 4096 | tf_op jit(solution)/shard_map/all_to_all | solution.py:64
  16.0 8.8 %all-to-all-start.1 = ((bf16[16,2,256]{2,1,0:T(2,128)(2,1)}), bf16[16,2,256]{2,1,0:T(2,128)(2,1)S(1)}, u32[]{:S(2)}, u32[]{:S(2)}) async-start(bf16[16,2,256]{2,1,0:T(2,128)(2,1)} %reshape.108), calls=%async_computation.1 | async-start | bytes 32768 | tf_op jit(solution)/shard_map/all_to_all | solution.py:63
  39.7 1.9 %copy-start = (f32[2,512,128,8]{2,1,3,0:T(8,128)}, f32[2,512,128,8]{2,1,3,0:T(8,128)S(1)}, u32[]{:S(2)}) copy-start(f32[2,512,128,8]{2,1,3,0:T(8,128)S(1)} %get-tuple-element.43) | copy-start | bytes 12582916 | tf_op jit(solution)/shard_map/cond
where the time goes:
time: 54.1 us; the launch traced here: 53.5 us
  blocking collectives  17 us (31%)
  starting transfers between devices  9.6 us (18%)
  local copies, waits for them, and re-layouts  7.91 us (15%)
  waiting for transfers between devices  7.34 us (14%)
  other arithmetic  5.85 us (11%)
  matrix products  5.05 us (9%)
  between operations  0.68 us (1%)
    all_to_all x1, starting transfers between devices, body(): lax.all_to_all(slot_place, 'dp', split_axis=0, concat_axis=0, tiled=True)  6.35 us
    all_gather x1, blocking collectives, body(): piece_values = lax.all_gather(merged_values, 'ctx', axis=0, tiled=True)  5.84 us
    all_gather x1, blocking collectives, body(): piece_keys = lax.all_gather(merged_keys, 'ctx', axis=0, tiled=True)  5.78 us
    psum x1, blocking collectives, body(): value_out = lax.psum(partial_value, 'tp')  5.42 us
    all_to_all x1, waiting for transfers between devices, body(): lax.all_to_all(slot_place, 'dp', split_axis=0, concat_axis=0, tiled=True)  3.85 us
    dot_general x1, matrix products, attend_block(): jnp.einsum('tgrs,sgd->tgrd', weights.astype(jnp.bfloat16), block_values,...  3.67 us
    all_to_all x1, waiting for transfers between devices, body(): lax.all_to_all(packed, 'dp', split_axis=0, concat_axis=0, tiled=True)  3.49 us
    all_to_all x1, starting transfers between devices, body(): lax.all_to_all(packed, 'dp', split_axis=0, concat_axis=0, tiled=True)  3.25 us
  transfers between devices with their start and end apart: 2, of which 2 were waited for; matrix products, arithmetic and copies ran while one was open for 7% of the time, Pallas kernels for 0%

commit v1 on v0

--- a/solution.py
+++ b/solution.py
@@ -1,10 +1,17 @@
+import functools
+import math
+
 import jax
 import jax.numpy as jnp
 from jax import lax
+from jax.experimental import pallas as pl
+from jax.experimental.pallas import tpu as pltpu
 from jax.sharding import PartitionSpec as P
 
 HD = 128
 CAP = 4
+SLOT_BYTES = 8 * 2**20
+MESH = pl.DeviceIdType.MESH
 
 
 def attend_block(
@@ -34,7 +41,7 @@
     return carried
 
 
-def body(queries, keys_text, values_text, patch_rows, patch_owner, patch_place, value_head):
+def collective_body(queries, keys_text, values_text, patch_rows, patch_owner, patch_place, value_head):
     token_count = queries.shape[1]
     kv_width = keys_text.shape[2]
     groups = kv_width // HD
@@ -112,6 +119,346 @@
     return (attention[None], value_out[None])
 
 
+def fused_kernel(
+    dp_count,
+    ctx_count,
+    tp_count,
+    code_ref,
+    rows_ref,
+    keys_ref,
+    values_ref,
+    probe_ref,
+    queries_hbm,
+    out_ref,
+    value_ref,
+    queries,
+    text,
+    rows_in,
+    code_in,
+    merged_keys,
+    merged_values,
+    probe,
+    partial,
+    partial_in,
+    query_sem,
+    local_sem,
+    text_send,
+    text_recv,
+    relay_send,
+    patch_send,
+    patch_recv,
+    value_send,
+    value_recv,
+):
+    d, c, t = lax.axis_index("dp"), lax.axis_index("ctx"), lax.axis_index("tp")
+    token_count, kv_width = keys_ref.shape
+    groups = kv_width // HD
+    heads = queries.shape[1] // HD
+    group_size = heads // groups
+    paired = ctx_count % 2 == 0
+    side = lax.rem(c, 2)
+    partner = c + 1 - 2 * side
+
+    load_queries = pltpu.make_async_copy(queries_hbm, queries, query_sem)
+    load_queries.start()
+    own_rows = pltpu.make_async_copy(rows_ref, rows_in.at[c, d], local_sem.at[0])
+    own_code = pltpu.make_async_copy(code_ref, code_in.at[c, d], local_sem.at[1])
+    own_rows.start()
+    own_code.start()
+
+    barrier = pltpu.get_barrier_semaphore()
+    for k in range(dp_count):
+        for m in range(ctx_count):
+            if k or m:
+                pl.semaphore_signal(
+                    barrier,
+                    inc=1,
+                    device_id=(lax.rem(d + k, dp_count), lax.rem(c + m, ctx_count), t),
+                    device_id_type=MESH,
+                )
+    for k in range(1, tp_count):
+        pl.semaphore_signal(
+            barrier, inc=1, device_id=(d, c, lax.rem(t + k, tp_count)), device_id_type=MESH
+        )
+    pl.semaphore_wait(barrier, dp_count * ctx_count - 1 + tp_count - 1)
+
+    def patch_copies(k, later):
+        there = lax.rem(d + k, dp_count)
+        return [
+            pltpu.make_async_remote_copy(
+                src_ref=src,
+                dst_ref=dst.at[c, d],
+                send_sem=patch_send.at[later, k, kind],
+                recv_sem=patch_recv.at[c, d, kind],
+                device_id=(there, later, t),
+                device_id_type=MESH,
+            )
+            for kind, (src, dst) in enumerate(((rows_ref, rows_in), (code_ref, code_in)))
+        ]
+
+    def text_copies(later):
+        return [
+            pltpu.make_async_remote_copy(
+                src_ref=src,
+                dst_ref=text.at[c, kind],
+                send_sem=text_send.at[later, kind],
+                recv_sem=text_recv.at[c, kind],
+                device_id=(d, later, t),
+                device_id_type=MESH,
+            )
+            for kind, src in enumerate((keys_ref, values_ref))
+        ]
+
+    def relay_copies(block):
+        return [
+            pltpu.make_async_remote_copy(
+                src_ref=text.at[block, kind],
+                dst_ref=text.at[block, kind],
+                send_sem=relay_send.at[block, kind],
+                recv_sem=text_recv.at[block, kind],
+                device_id=(d, partner, t),
+                device_id_type=MESH,
+            )
+            for kind in range(2)
+        ]
+
+    def sends_text(later):
+        if not paired:
+            return c < later
+        return (c < later) & ((side == later % 2) | (partner == later))
+
+    def for_patches(act):
+        for k in range(dp_count):
+            for later in range(ctx_count):
+                reached = (c < later) if k == 0 else (c <= later)
+
+                @pl.when(reached)
+                def _():
+                    for copy in patch_copies(k, later):
+                        act(copy)
+
+    def for_text(act):
+        for later in range(1, ctx_count):
+
+            @pl.when(sends_text(later))
+            def _():
+                for copy in text_copies(later):
+                    act(copy)
+
+    for_patches(lambda copy: copy.start())
+    for_text(lambda copy: copy.start())
+
+    probe[...] = probe_ref[...].astype(jnp.float32)
+    own_rows.wait()
+    own_code.wait()
+
+    def wait_text(block):
+        for copy in relay_copies(block):
+            copy.wait_recv()
+
+    def wait_patches(block, first):
+        for k in range(first, dp_count):
+            there = lax.rem(d + k, dp_count)
+            for kind, (src, dst) in enumerate(((rows_ref, rows_in), (code_ref, code_in))):
+                pltpu.make_async_remote_copy(
+                    src_ref=src,
+                    dst_ref=dst.at[block, there],
+                    send_sem=patch_send.at[0, k, kind],
+                    recv_sem=patch_recv.at[block, there, kind],
+                    device_id=(there, c, t),
+                    device_id_type=MESH,
+                ).wait_recv()
+
+    def merge(block, block_keys, block_values):
+        slots = dp_count * rows_ref.shape[0]
+        code = code_in[block].reshape(slots, 1)
+        rows = rows_in[block].astype(jnp.float32).reshape(slots, 2 * kv_width)
+        spots = d * token_count + lax.broadcasted_iota(jnp.int32, (slots, token_count), 1)
+        landing = jnp.where(code == spots, 1.0, 0.0).astype(jnp.bfloat16)
+        arrivals = lax.dot_general(
+            landing,
+            rows.astype(jnp.bfloat16),
+            (((0,), (0,)), ((), ())),
+            preferred_element_type=jnp.float32,
+        )
+        span = pl.ds(block * token_count, token_count)
+        merged_keys[span, :] = (
+            block_keys.astype(jnp.float32) + arrivals[:, :kv_width]
+        ).astype(jnp.bfloat16)
+        merged_values[span, :] = (
+            block_values.astype(jnp.float32) + arrivals[:, kv_width:]
+        ).astype(jnp.bfloat16)
+
+    if paired:
+        for block in range(ctx_count - 2):
+
+            @pl.when((block < c) & (side == block % 2))
+            def _():
+                wait_text(block)
+
+                @pl.when(block < c - side)
+                def _():
+                    for copy in relay_copies(block):
+                        copy.start()
+
+    for block in range(ctx_count):
+
+        @pl.when(block == c)
+        def _():
+            wait_patches(block, 1)
+            merge(block, keys_ref[...], values_ref[...])
+
+        @pl.when(block < c)
+        def _():
+            wait_patches(block, 0)
+            if paired:
+
+                @pl.when(side != block % 2)
+                def _():
+                    wait_text(block)
+
+            else:
+                wait_text(block)
+            merge(block, text[block, 0], text[block, 1])
+
+    load_queries.wait()
+    score_scale = HD ** (-0.5) * math.log2(math.e)
+
+    def attend(last):
+        length = (last + 1) * token_count
+        row = lax.broadcasted_iota(jnp.int32, (token_count, token_count), 0)
+        col = lax.broadcasted_iota(jnp.int32, (token_count, token_count), 1)
+        allowed = col <= row
+        unroll = math.gcd(group_size, 4)
+
+        def step(number, total):
+            first = number * unroll
+            lane = pl.multiple_of((first // group_size) * HD, HD)
+            block_keys = merged_keys[0:length, pl.ds(lane, HD)]
+            block_values = merged_values[0:length, pl.ds(lane, HD)]
+            for extra in range(unroll):
+                head = first + extra
+                place = pl.ds(pl.multiple_of(head * HD, HD), HD)
+                scores = lax.dot_general(
+                    queries[:, place],
+                    block_keys,
+                    (((1,), (1,)), ((), ())),
+                    preferred_element_type=jnp.float32,
+                )
+                parts = [
+                    scores[:, j * token_count : (j + 1) * token_count] for j in range(last + 1)
+                ]
+                parts[last] = jnp.where(allowed, parts[last], -1e30)
+                top = functools.reduce(jnp.maximum, parts)
+                top = jnp.max(top, axis=1, keepdims=True)
+                weights = [jnp.exp2((part - top) * score_scale) for part in parts]
+                denominator = jnp.sum(
+                    functools.reduce(jnp.add, weights), axis=1, keepdims=True
+                )
+                rounded = jnp.concatenate([w.astype(jnp.bfloat16) for w in weights], axis=1)
+                numerator = jnp.dot(rounded, block_values, preferred_element_type=jnp.float32)
+                result = (numerator * (1.0 / denominator)).astype(jnp.bfloat16)
+                out_ref[:, place] = result
+                total = total + result.astype(jnp.float32) * probe[pl.ds(head, 1), :]
+            return total
+
+        total = lax.fori_loop(
+            0, heads // unroll, step, jnp.zeros((token_count, HD), jnp.float32)
+        )
+        partial[...] = jnp.sum(jnp.transpose(total), axis=0, keepdims=True)
+
+    for last in range(ctx_count):
+
+        @pl.when(c == last)
+        def _():
+            attend(last)
+
+    value_copies = [
+        pltpu.make_async_remote_copy(
+            src_ref=partial,
+            dst_ref=partial_in.at[k - 1],
+            send_sem=value_send.at[k - 1],
+            recv_sem=value_recv.at[k - 1],
+            device_id=(d, c, lax.rem(t + k, tp_count)),
+            device_id_type=MESH,
+        )
+        for k in range(1, tp_count)
+    ]
+    for copy in value_copies:
+        copy.start()
+    for_patches(lambda copy: copy.wait_send())
+    for_text(lambda copy: copy.wait_send())
+    if paired:
+        for block in range(ctx_count - 2):
+
+            @pl.when((block < c - side) & (side == block % 2))
+            def _():
+                for copy in relay_copies(block):
+                    copy.wait_send()
+
+    for copy in value_copies:
+        copy.wait()
+    whole = partial[...]
+    for k in range(1, tp_count):
+        whole = whole + partial_in[k - 1]
+    value_ref[...] = whole
+
+
+def fused_body(sizes, queries, keys_text, values_text, patch_rows, patch_owner, patch_place, value_head):
+    dp_count, ctx_count, tp_count = sizes
+    _, token_count, query_width = queries.shape
+    kv_width = keys_text.shape[2]
+    row_count = patch_rows.shape[2]
+    heads = query_width // HD
+    code = patch_owner[0, 0] * token_count + patch_place[0, 0][:, None]
+    rows = patch_rows[0, 0].reshape(row_count, 2 * kv_width)
+    dma = pltpu.SemaphoreType.DMA
+    vmem = pl.BlockSpec(memory_space=pltpu.VMEM)
+    attention, value_out = pl.pallas_call(
+        functools.partial(fused_kernel, dp_count, ctx_count, tp_count),
+        out_shape=(
+            jax.ShapeDtypeStruct((token_count, query_width), jnp.bfloat16),
+            jax.ShapeDtypeStruct((1, token_count), jnp.float32),
+        ),
+        in_specs=[vmem] * 5 + [pl.BlockSpec(memory_space=pl.ANY)],
+        out_specs=(vmem, vmem),
+        scratch_shapes=[
+            pltpu.VMEM((token_count, query_width), jnp.bfloat16),
+            pltpu.VMEM((ctx_count, 2, token_count, kv_width), jnp.bfloat16),
+            pltpu.VMEM((ctx_count, dp_count, row_count, 2 * kv_width), jnp.bfloat16),
+            pltpu.VMEM((ctx_count, dp_count, row_count, 1), jnp.int32),
+            pltpu.VMEM((ctx_count * token_count, kv_width), jnp.bfloat16),
+            pltpu.VMEM((ctx_count * token_count, kv_width), jnp.bfloat16),
+            pltpu.VMEM((heads, HD), jnp.float32),
+            pltpu.VMEM((1, token_count), jnp.float32),
+            pltpu.VMEM((max(tp_count - 1, 1), 1, token_count), jnp.float32),
+            dma,
+            dma((2,)),
+            dma((ctx_count, 2)),
+            dma((ctx_count, 2)),
+            dma((ctx_count, 2)),
+            dma((ctx_count, dp_count, 2)),
+            dma((ctx_count, dp_count, 2)),
+            dma((max(tp_count - 1, 1),)),
+            dma((max(tp_count - 1, 1),)),
+        ],
+        compiler_params=pltpu.CompilerParams(
+            collective_id=0, has_side_effects=True, vmem_limit_bytes=48 * 2**20
+        ),
+        name="merged_attention",
+    )(code, rows, keys_text[0], values_text[0], value_head.reshape(heads, HD), queries[0])
+    return (attention[None], value_out)
+
+
+def body(sizes, queries, keys_text, values_text, patch_rows, patch_owner, patch_place, value_head):
+    dp_count, ctx_count, _ = sizes
+    arriving = dp_count * ctx_count * patch_rows.size * patch_rows.dtype.itemsize
+    arrays = (queries, keys_text, values_text, patch_rows, patch_owner, patch_place, value_head)
+    if arriving > SLOT_BYTES:
+        return collective_body(*arrays)
+    return fused_body(sizes, *arrays)
+
+
 def solution(mesh):
     in_specs = (
         P("dp", "ctx", "tp"),
@@ -123,4 +470,11 @@
         P("tp"),
     )
     out_specs = (P("dp", "ctx", "tp"), P("dp", "ctx"))
-    return jax.shard_map(body, mesh=mesh, in_specs=in_specs, out_specs=out_specs, check_vma=False)
+    sizes = tuple(mesh.shape[axis] for axis in ("dp", "ctx", "tp"))
+    return jax.shard_map(
+        functools.partial(body, sizes),
+        mesh=mesh,
+        in_specs=in_specs,
+        out_specs=out_specs,
+        check_vma=False,
+    )

time: 54.1 us -> 29.4 us (0.54)
  the two profiles are of different devices: /device:TPU:0 before, /device:TPU:5 now
where the time goes in v1:
time: 29.4 us; the launch traced here: 29 us
  Pallas kernels  21.7 us (74%)
  local copies, waits for them, and re-layouts  6.7 us (23%)
  between operations  0.66 us (2%)
    pallas_call x1, Pallas kernels, fused_body(): pl.pallas_call(functools.partial(fused_kernel, dp_count, ctx_count, tp_co...  21.7 us
    unnamed x17, local copies, waits for them, and re-layouts  6.54 us

profile of v1, /device:TPU:5, one launch (start us, length us, event | category | flops | bytes accessed | tf_op | source)
XLA Modules:
  0.0 29.0 jit_solution(12528439272494832059)
XLA Ops:
  0.6 0.0 copy-start.6
  0.6 0.6 %copy-done.6 = s32[1,1,8,1]{2,3,1,0:T(1,128)S(1)} copy-done((s32[1,1,8,1]{2,3,1,0:T(1,128)S(1)}, s32[1,1,8,1]{2,3,1,0:T(1,128)}, u32[]{:S(2)}) %copy-start.6) | copy-done | bytes 56
  1.3 0.0 copy-start.5
  1.3 0.1 copy.9
  1.4 0.6 %copy-done.5 = s32[1,1,8]{2,1,0:T(1,128)S(1)} copy-done((s32[1,1,8]{2,1,0:T(1,128)S(1)}, s32[1,1,8]{2,1,0:T(1,128)}, u32[]{:S(2)}) %copy-start.5) | copy-done | bytes 56
  1.9 0.0 copy-start.4
  1.9 0.1 copy.10
  2.0 0.6 %copy-done.4 = bf16[1,1,8,2,256]{4,3,2,1,0:T(2,128)(2,1)S(1)} copy-done((bf16[1,1,8,2,256]{4,3,2,1,0:T(2,128)(2,1)S(1)}, bf16[1,1,8,2,256]{4,3,2,1,0:T(2,128)(2,1)}, u32[]{:S(2)}) %copy-start.4) | copy-done | bytes 8216
  2.6 0.0 copy-start.3
  2.6 0.7 %copy-done.3 = bf16[2048]{0:T(1024)(128)(2,1)S(1)} copy-done((bf16[2048]{0:T(1024)(128)(2,1)S(1)}, bf16[2048]{0:T(1024)(128)(2,1)}, u32[]{:S(2)}) %copy-start.3) | copy-done | bytes 4120
  3.3 0.0 copy-start
  3.3 1.0 %copy-done = bf16[1,128,2048]{2,1,0:T(8,128)(2,1)S(1)} copy-done((bf16[1,128,2048]{2,1,0:T(8,128)(2,1)S(1)}, bf16[1,128,2048]{2,1,0:T(8,128)(2,1)}, u32[]{:S(2)}) %copy-start) | copy-done | bytes 524312
  4.4 0.0 copy-start.1
  4.4 0.8 %copy-done.1 = bf16[1,128,256]{2,1,0:T(8,128)(2,1)S(1)} copy-done((bf16[1,128,256]{2,1,0:T(8,128)(2,1)S(1)}, bf16[1,128,256]{2,1,0:T(8,128)(2,1)}, u32[]{:S(2)}) %copy-start.1) | copy-done | bytes 65560
  5.2 0.0 copy-start.2
  5.2 0.8 %copy-done.2 = bf16[1,128,256]{2,1,0:T(8,128)(2,1)S(1)} copy-done((bf16[1,128,256]{2,1,0:T(8,128)(2,1)S(1)}, bf16[1,128,256]{2,1,0:T(8,128)(2,1)}, u32[]{:S(2)}) %copy-start.2) | copy-done | bytes 65560
  6.1 21.7 %merged_attention.1 = (bf16[128,2048]{1,0:T(8,128)(2,1)S(1)}, f32[1,128]{1,0:T(1,128)S(1)}) custom-call(s32[8,1]{1,0:T(8,128)S(1)} %add.3.code_ref, bf16[8,512]{1,0:T(8,128)(2,1)S(1)} %bitcast.15, bf16[128,256]{1,0:T(8,128)(2,1)S(1)} %bitcast.13, bf16[128,256]{1,0:T(8,128)(2,1)S(1)} %bitcast.14, bf16[16,128]{1,0:T(8,128)(2,1)S(1)} %bitcast.16, ...), custom_call_target="tpu_custom_call" | custom-call | tf_op jit(solution)/shard_map/merged_attention/pallas_call | solution.py:417
  27.7 0.8 %copy.14 = bf16[1,128,2048]{2,1,0:T(8,128)(2,1)} copy(bf16[1,128,2048]{2,1,0:T(8,128)(2,1)S(1)} %bitcast.12) | data formatting | bytes 1048576
  28.5 0.5 %copy.15 = f32[1,128]{1,0:T(1,128)} copy(f32[1,128]{1,0:T(1,128)S(1)} %get-tuple-element.9) | data formatting | bytes 1024
  (3 shorter events, 0.0 us)
Async XLA Ops:
  0.6 0.7 %copy-start.6 = (s32[1,1,8,1]{2,3,1,0:T(1,128)S(1)}, s32[1,1,8,1]{2,3,1,0:T(1,128)}, u32[]{:S(2)}) copy-start(s32[1,1,8,1]{2,3,1,0:T(1,128)} %param.11) | copy-start | bytes 100
  1.3 0.7 %copy-start.5 = (s32[1,1,8]{2,1,0:T(1,128)S(1)}, s32[1,1,8]{2,1,0:T(1,128)}, u32[]{:S(2)}) copy-start(s32[1,1,8]{2,1,0:T(1,128)} %param.12) | copy-start | bytes 100
  1.9 0.7 %copy-start.4 = (bf16[1,1,8,2,256]{4,3,2,1,0:T(2,128)(2,1)S(1)}, bf16[1,1,8,2,256]{4,3,2,1,0:T(2,128)(2,1)}, u32[]{:S(2)}) copy-start(bf16[1,1,8,2,256]{4,3,2,1,0:T(2,128)(2,1)} %param.10) | copy-start | bytes 24580
  2.6 0.7 %copy-start.3 = (bf16[2048]{0:T(1024)(128)(2,1)S(1)}, bf16[2048]{0:T(1024)(128)(2,1)}, u32[]{:S(2)}) copy-start(bf16[2048]{0:T(1024)(128)(2,1)} %param.13) | copy-start | bytes 12292
  3.3 1.0 %copy-start = (bf16[1,128,2048]{2,1,0:T(8,128)(2,1)S(1)}, bf16[1,128,2048]{2,1,0:T(8,128)(2,1)}, u32[]{:S(2)}) copy-start(bf16[1,128,2048]{2,1,0:T(8,128)(2,1)} %param.7) | copy-start | bytes 1572868
  4.4 0.8 %copy-start.1 = (bf16[1,128,256]{2,1,0:T(8,128)(2,1)S(1)}, bf16[1,128,256]{2,1,0:T(8,128)(2,1)}, u32[]{:S(2)}) copy-start(bf16[1,128,256]{2,1,0:T(8,128)(2,1)} %param.8) | copy-start | bytes 196612
  5.2 0.8 %copy-start.2 = (bf16[1,128,256]{2,1,0:T(8,128)(2,1)S(1)}, bf16[1,128,256]{2,1,0:T(8,128)(2,1)}, u32[]{:S(2)}) copy-start(bf16[1,128,256]{2,1,0:T(8,128)(2,1)} %param.9) | copy-start | bytes 196612

commit v2 on v1

--- a/solution.py
+++ b/solution.py
@@ -123,20 +123,22 @@
     dp_count,
     ctx_count,
     tp_count,
-    code_ref,
-    rows_ref,
-    keys_ref,
-    values_ref,
-    probe_ref,
+    owner_hbm,
+    place_hbm,
+    rows_hbm,
+    keys_hbm,
+    values_hbm,
+    probe_hbm,
     queries_hbm,
     out_ref,
     value_ref,
     queries,
     text,
     rows_in,
-    code_in,
+    spots_in,
     merged_keys,
     merged_values,
+    probe_raw,
     probe,
     partial,
     partial_in,
@@ -151,20 +153,13 @@
     value_recv,
 ):
     d, c, t = lax.axis_index("dp"), lax.axis_index("ctx"), lax.axis_index("tp")
-    token_count, kv_width = keys_ref.shape
+    token_count, kv_width = keys_hbm.shape
     groups = kv_width // HD
     heads = queries.shape[1] // HD
     group_size = heads // groups
     paired = ctx_count % 2 == 0
     side = lax.rem(c, 2)
     partner = c + 1 - 2 * side
-
-    load_queries = pltpu.make_async_copy(queries_hbm, queries, query_sem)
-    load_queries.start()
-    own_rows = pltpu.make_async_copy(rows_ref, rows_in.at[c, d], local_sem.at[0])
-    own_code = pltpu.make_async_copy(code_ref, code_in.at[c, d], local_sem.at[1])
-    own_rows.start()
-    own_code.start()
 
     barrier = pltpu.get_barrier_semaphore()
     for k in range(dp_count):
@@ -180,33 +175,54 @@
         pl.semaphore_signal(
             barrier, inc=1, device_id=(d, c, lax.rem(t + k, tp_count)), device_id_type=MESH
         )
+
+    loads = [
+        pltpu.make_async_copy(src, dst, local_sem.at[number])
+        for number, (src, dst) in enumerate(
+            (
+                (rows_hbm, rows_in.at[c, d]),
+                (owner_hbm, spots_in.at[c, d, 0]),
+                (place_hbm, spots_in.at[c, d, 1]),
+                (keys_hbm, text.at[c, 0]),
+                (values_hbm, text.at[c, 1]),
+                (probe_hbm, probe_raw),
+            )
+        )
+    ]
+    load_queries = pltpu.make_async_copy(queries_hbm, queries, query_sem)
+    for load in loads:
+        load.start()
+    load_queries.start()
+    for load in loads:
+        load.wait()
+    probe[...] = probe_raw[...].astype(jnp.float32)
     pl.semaphore_wait(barrier, dp_count * ctx_count - 1 + tp_count - 1)
 
     def patch_copies(k, later):
         there = lax.rem(d + k, dp_count)
         return [
             pltpu.make_async_remote_copy(
-                src_ref=src,
-                dst_ref=dst.at[c, d],
+                src_ref=part.at[c, d],
+                dst_ref=part.at[c, d],
                 send_sem=patch_send.at[later, k, kind],
                 recv_sem=patch_recv.at[c, d, kind],
                 device_id=(there, later, t),
                 device_id_type=MESH,
             )
-            for kind, (src, dst) in enumerate(((rows_ref, rows_in), (code_ref, code_in)))
+            for kind, part in enumerate((rows_in, spots_in))
         ]
 
     def text_copies(later):
         return [
             pltpu.make_async_remote_copy(
-                src_ref=src,
+                src_ref=text.at[c, kind],
                 dst_ref=text.at[c, kind],
                 send_sem=text_send.at[later, kind],
                 recv_sem=text_recv.at[c, kind],
                 device_id=(d, later, t),
                 device_id_type=MESH,
             )
-            for kind, src in enumerate((keys_ref, values_ref))
+            for kind in range(2)
         ]
 
     def relay_copies(block):
@@ -248,10 +264,6 @@
     for_patches(lambda copy: copy.start())
     for_text(lambda copy: copy.start())
 
-    probe[...] = probe_ref[...].astype(jnp.float32)
-    own_rows.wait()
-    own_code.wait()
-
     def wait_text(block):
         for copy in relay_copies(block):
             copy.wait_recv()
@@ -259,35 +271,34 @@
     def wait_patches(block, first):
         for k in range(first, dp_count):
             there = lax.rem(d + k, dp_count)
-            for kind, (src, dst) in enumerate(((rows_ref, rows_in), (code_ref, code_in))):
+            for kind, part in enumerate((rows_in, spots_in)):
                 pltpu.make_async_remote_copy(
-                    src_ref=src,
-                    dst_ref=dst.at[block, there],
+                    src_ref=part.at[block, there],
+                    dst_ref=part.at[block, there],
                     send_sem=patch_send.at[0, k, kind],
                     recv_sem=patch_recv.at[block, there, kind],
                     device_id=(there, c, t),
                     device_id_type=MESH,
                 ).wait_recv()
 
-    def merge(block, block_keys, block_values):
-        slots = dp_count * rows_ref.shape[0]
-        code = code_in[block].reshape(slots, 1)
-        rows = rows_in[block].astype(jnp.float32).reshape(slots, 2 * kv_width)
-        spots = d * token_count + lax.broadcasted_iota(jnp.int32, (slots, token_count), 1)
-        landing = jnp.where(code == spots, 1.0, 0.0).astype(jnp.bfloat16)
-        arrivals = lax.dot_general(
-            landing,
-            rows.astype(jnp.bfloat16),
-            (((0,), (0,)), ((), ())),
-            preferred_element_type=jnp.float32,
-        )
+    def merge(block):
+        slots = dp_count * rows_hbm.shape[0]
+        spots = spots_in[block]
+        code = spots[:, 0] * token_count + spots[:, 1]
+        code = jnp.concatenate([code[k] for k in range(dp_count)], axis=1)
+        here = d * token_count + lax.broadcasted_iota(jnp.int32, (token_count, slots), 0)
+        landing = jnp.where(code == here, 1.0, 0.0).astype(jnp.bfloat16)
+        rows = rows_in[block].astype(jnp.float32)
+        row_keys = rows[:, :, 0, :].reshape(slots, kv_width).astype(jnp.bfloat16)
+        row_values = rows[:, :, 1, :].reshape(slots, kv_width).astype(jnp.bfloat16)
         span = pl.ds(block * token_count, token_count)
-        merged_keys[span, :] = (
-            block_keys.astype(jnp.float32) + arrivals[:, :kv_width]
-        ).astype(jnp.bfloat16)
-        merged_values[span, :] = (
-            block_values.astype(jnp.float32) + arrivals[:, kv_width:]
-        ).astype(jnp.bfloat16)
+        for kind, (rows, merged) in enumerate(
+            ((row_keys, merged_keys), (row_values, merged_values))
+        ):
+            arrivals = jnp.dot(landing, rows, preferred_element_type=jnp.float32)
+            merged[span, :] = (text[block, kind].astype(jnp.float32) + arrivals).astype(
+                jnp.bfloat16
+            )
 
     if paired:
         for block in range(ctx_count - 2):
@@ -306,7 +317,7 @@
         @pl.when(block == c)
         def _():
             wait_patches(block, 1)
-            merge(block, keys_ref[...], values_ref[...])
+            merge(block)
 
         @pl.when(block < c)
         def _():
@@ -319,7 +330,7 @@
 
             else:
                 wait_text(block)
-            merge(block, text[block, 0], text[block, 1])
+            merge(block)
 
     load_queries.wait()
     score_scale = HD ** (-0.5) * math.log2(math.e)
@@ -410,8 +421,6 @@
     kv_width = keys_text.shape[2]
     row_count = patch_rows.shape[2]
     heads = query_width // HD
-    code = patch_owner[0, 0] * token_count + patch_place[0, 0][:, None]
-    rows = patch_rows[0, 0].reshape(row_count, 2 * kv_width)
     dma = pltpu.SemaphoreType.DMA
     vmem = pl.BlockSpec(memory_space=pltpu.VMEM)
     attention, value_out = pl.pallas_call(
@@ -420,20 +429,21 @@
             jax.ShapeDtypeStruct((token_count, query_width), jnp.bfloat16),
             jax.ShapeDtypeStruct((1, token_count), jnp.float32),
         ),
-        in_specs=[vmem] * 5 + [pl.BlockSpec(memory_space=pl.ANY)],
+        in_specs=[pl.BlockSpec(memory_space=pltpu.HBM)] * 7,
         out_specs=(vmem, vmem),
         scratch_shapes=[
             pltpu.VMEM((token_count, query_width), jnp.bfloat16),
             pltpu.VMEM((ctx_count, 2, token_count, kv_width), jnp.bfloat16),
-            pltpu.VMEM((ctx_count, dp_count, row_count, 2 * kv_width), jnp.bfloat16),
-            pltpu.VMEM((ctx_count, dp_count, row_count, 1), jnp.int32),
+            pltpu.VMEM((ctx_count, dp_count, row_count, 2, kv_width), jnp.bfloat16),
+            pltpu.VMEM((ctx_count, dp_count, 2, 1, row_count), jnp.int32),
             pltpu.VMEM((ctx_count * token_count, kv_width), jnp.bfloat16),
             pltpu.VMEM((ctx_count * token_count, kv_width), jnp.bfloat16),
+            pltpu.VMEM((heads, HD), jnp.bfloat16),
             pltpu.VMEM((heads, HD), jnp.float32),
             pltpu.VMEM((1, token_count), jnp.float32),
             pltpu.VMEM((max(tp_count - 1, 1), 1, token_count), jnp.float32),
             dma,
-            dma((2,)),
+            dma((6,)),
             dma((ctx_count, 2)),
             dma((ctx_count, 2)),
             dma((ctx_count, 2)),
@@ -443,10 +453,18 @@
             dma((max(tp_count - 1, 1),)),
         ],
         compiler_params=pltpu.CompilerParams(
-            collective_id=0, has_side_effects=True, vmem_limit_bytes=48 * 2**20
+            collective_id=0, has_side_effects=True, vmem_limit_bytes=67043328
         ),
         name="merged_attention",
-    )(code, rows, keys_text[0], values_text[0], value_head.reshape(heads, HD), queries[0])
+    )(
+        patch_owner[0, 0].reshape(1, row_count),
+        patch_place[0],
+        patch_rows[0, 0],
+        keys_text[0],
+        values_text[0],
+        value_head.reshape(heads, HD),
+        queries[0],
+    )
     return (attention[None], value_out)
 
 

time: 29.4 us -> 25.1 us (0.85)
  local copies, waits for them, and re-layouts: 6.7 us -> 2.4 us
    unnamed x17 -> x4, local copies, waits for them, and re-layouts: 6.54 us -> 2.4 us
where the time goes in v2:
time: 25.1 us; the launch traced here: 24.9 us
  Pallas kernels  21.9 us (87%)
  local copies, waits for them, and re-layouts  2.4 us (10%)
  between operations  0.65 us (3%)
    pallas_call x1, Pallas kernels, fused_body(): pl.pallas_call(functools.partial(fused_kernel, dp_count, ctx_count, tp_co...  21.9 us
    unnamed x4, local copies, waits for them, and re-layouts  2.4 us

profile of v2, /device:TPU:5, one launch (start us, length us, event | category | flops | bytes accessed | tf_op | source)
XLA Modules:
  0.0 24.9 jit_solution(10578577328938108616)
XLA Ops:
  0.6 21.9 %merged_attention.1 = (bf16[128,2048]{1,0:T(8,128)(2,1)}, f32[1,128]{1,0:T(1,128)}) custom-call(s32[1,8]{1,0:T(1,128)} %bitcast.14, s32[1,8]{1,0:T(1,128)} %bitcast.15, bf16[8,2,256]{2,1,0:T(2,128)(2,1)} %bitcast.12, bf16[128,256]{1,0:T(8,128)(2,1)} %bitcast.10, bf16[128,256]{1,0:T(8,128)(2,1)} %bitcast.11, bf16[16,128]{1,0:T(8,128)(2,1)} %bitcast.13, ...), custom_call_target="tpu_custom_call" | custom-call | tf_op jit(solution)/shard_map/merged_attention/pallas_call | solution.py:426
  22.5 0.0 copy-start
  22.5 1.9 %copy.11 = bf16[1,128,2048]{2,1,0:T(8,128)(2,1)} copy(bf16[1,128,2048]{2,1,0:T(8,128)(2,1)} %bitcast.9) | data formatting | bytes 1048576
  24.4 0.0 copy-done
  24.4 0.5 %copy.12 = f32[1,128]{1,0:T(1,128)} copy(f32[1,128]{1,0:T(1,128)S(1)} %copy-done) | data formatting | bytes 1024
Async XLA Ops:
  22.5 1.9 %copy-start = (f32[1,128]{1,0:T(1,128)S(1)}, f32[1,128]{1,0:T(1,128)}, u32[]{:S(2)}) copy-start(f32[1,128]{1,0:T(1,128)} %get-tuple-element.9) | copy-start | bytes 1540
